TPU v7x, 32 devices: a whole 2x2x4 slice. The times are simulated.
32 devices in a mesh: train: 2 (over y), tp: 8 (over z, x), dp: 2 (over core).
Axes of the slice: x: 2, y: 2, z: 4, core: 2. Of those that a mesh axis runs over, the one named last changes fastest.
Arguments:
- adapter_down_factor: bfloat16 [2, 2, 64, 8192], P(None, None, None, ('train', 'tp')), may hold values from -6 to 6
- adapter_up_factor: bfloat16 [2, 2, 1024, 64], P(None, None, ('train', 'tp')), may hold values from -0.75 to 0.75
- projection_weight: bfloat16 [2, 2, 1024, 8192], P(None, None, 'tp'), may hold values from -6 to 6
Outputs:
- merged: bfloat16 [2, 2, 1024, 8192], P(None, None, 'tp')
All inputs are finite; a program needn't handle non-finite values.
Results may differ from a plain program's by a relative error of at most 0.001.
Values may be sent and summed in bfloat16 or wider, within the bound.
A program may use at most 64 MiB of HBM per device.

v0:
```python
import jax
import jax.numpy as jnp
from jax import lax
from jax.sharding import PartitionSpec as P

adapter_scale = 2.0


def per_device(adapter_down_factor, adapter_up_factor, projection_weight):
    per_rows = projection_weight.shape[2]
    all_up_factors = lax.all_gather(adapter_up_factor, ("train", "tp"), axis=2, tiled=True)
    offset = lax.axis_index("tp") * per_rows
    b_rows = lax.dynamic_slice_in_dim(all_up_factors, offset, per_rows, 2)
    weight_block = projection_weight.astype(jnp.float32)
    weight_update = jnp.einsum(
        "eitd,eidh->eith",
        b_rows,
        lax.all_gather(adapter_down_factor, ("train", "tp"), axis=3, tiled=True),
        preferred_element_type=jnp.float32,
    )
    return (weight_block + adapter_scale * weight_update).astype(jnp.bfloat16)


def solution(mesh):
    in_specs = (
        P(None, None, None, ("train", "tp")),
        P(None, None, ("train", "tp"), None),
        P(None, None, "tp", None),
    )
    out_specs = P(None, None, "tp", None)
    return jax.shard_map(
        per_device, mesh=mesh, in_specs=in_specs, out_specs=out_specs, check_vma=False
    )
```

profile of v0, /device:TPU:0, one launch (start us, length us, event | category | flops | bytes accessed | tf_op | source)
XLA Modules:
  0.0 113.6 jit_solution(2396535174543031142)
XLA Ops:
  6.5 0.0 all-gather.2.cloned.1.call-start
  6.5 0.7 all-gather.2.cloned.1.call-update
  7.3 0.9 copy.5
  8.2 51.4 %all_gather.6 = bf16[2,2,1024,64]{3,1,0,2:T(2,128)(2,1)S(1)} all-gather(bf16[2,2,64,64]{3,1,0,2:T(2,128)(2,1)S(1)} %copy.5), channel_id=1, replica_groups=mesh['train'=2,'tp'=8,'dp'=2] {'train','tp'}, dimensions={2}, use_global_device_ids=true | all-gather | bytes 557056 | tf_op jit(solution)/shard_map/all_gather | solution.py:11
  59.5 0.1 constant_dynamic-slice_fusion
  59.6 39.0 %all-gather.2.cloned.1.call-done = bf16[2,2,64,8192]{3,2,1,0:T(8,128)(2,1)} async-done(((bf16[2,2,64,512]{3,2,1,0:T(8,128)(2,1)}), bf16[2,2,64,8192]{3,2,1,0:T(8,128)(2,1)}) %all-gather.2.cloned.1.call-update) | async-done | bytes 4194320 | tf_op jit(solution)/shard_map/all_gather | solution.py:18
  98.6 8.2 %add_convert_fusion = bf16[2,2,128,8192]{3,2,1,0:T(8,128)(2,1)} fusion(bf16[2,2,128,8192]{3,2,1,0:T(8,128)(2,1)} %param.5, bf16[2,2,64,8192]{3,2,1,0:T(8,128)(2,1)} %all-gather.2.cloned.1.call-done, bf16[2,2,128,64]{3,1,0,2:T(2,128)(2,1)S(1)} %constant_dynamic-slice_fusion), kind=kOutput, calls=%fused_computation | convolution fusion | flops 553648128 | bytes 21037056 | tf_op jit(solution)/shard_map/eitd,eidh->eith/dot_general | solution.py:15
Async XLA Ops:
  6.5 92.0 %all-gather.2.cloned.1.call-start = ((), (), s32[]{:S(2)}) async-start(), calls=%async_computation | async-start | bytes 4456448 | tf_op jit(solution)/shard_map/all_gather | solution.py:18
Sparse Core Ops, SparseCore 0:
  10.1 88.4 all-gather.1
where the time goes:
time: 114 us
  blocking collectives  51.4 us (45%)
  waiting for transfers between devices  39.7 us (35%)
  between operations  13.4 us (12%)
  matrix products  8.17 us (7%)
    all_gather x1, blocking collectives, per_device(): lax.all_gather(adapter_up_factor, ('train', 'tp'), axis=2, tiled=True)  51.4 us
    all_gather x1, waiting for transfers between devices, per_device(): lax.all_gather(adapter_down_factor, ('train', 'tp'), axis=3, tiled=True)  39 us
    dot_general x1, matrix products, per_device(): jnp.einsum('eitd,eidh->eith', b_rows, lax.all_gather(adapter_down_factor,...  8.17 us
  transfers between devices with their start and end apart: 1, of which 1 were waited for; matrix products, arithmetic and copies ran while one was open for 1% of the time, Pallas kernels for 0%

commit v1 on v0

--- a/solution.py
+++ b/solution.py
@@ -4,6 +4,10 @@
 from jax.sharding import PartitionSpec as P
 
 adapter_scale = 2.0
+
+
+def build_shards(slab_in, which_axis):
+    return jnp.concatenate(lax.all_gather(slab_in, which_axis), axis=3)
 
 
 def per_device(adapter_down_factor, adapter_up_factor, projection_weight):
@@ -15,7 +19,7 @@
     weight_update = jnp.einsum(
         "eitd,eidh->eith",
         b_rows,
-        lax.all_gather(adapter_down_factor, ("train", "tp"), axis=3, tiled=True),
+        build_shards(adapter_down_factor, ("train", "tp")),
         preferred_element_type=jnp.float32,
     )
     return (weight_block + adapter_scale * weight_update).astype(jnp.bfloat16)

time: 114 us -> 123 us (1.079)
  local copies, waits for them, and re-layouts: 1 us -> 15 us
  waiting for transfers between devices: 39.7 us -> 33.1 us
  blocking collectives: 51.4 us -> 53.2 us
    reshape x0 -> x1, local copies, waits for them, and re-layouts: none -> 7.38 us  [build_shards(): return jnp.concatenate(lax.all_gather(slab_in, which_axis), axis=3)]
    all_gather x1, waiting for transfers between devices: 39 us -> 32.4 us  [build_shards(): return jnp.concatenate(lax.all_gather(slab_in, which_axis), axis=3)]
    all_gather x0 -> x1, local copies, waits for them, and re-layouts: none -> 6.59 us  [build_shards(): return jnp.concatenate(lax.all_gather(slab_in, which_axis), axis=3)]
    all_gather x1, blocking collectives: 51.4 us -> 53.2 us  [per_device(): lax.all_gather(adapter_up_factor, ('train', 'tp'), axis=2, tiled=True)]
where the time goes in v1:
time: 123 us
  blocking collectives  53.2 us (43%)
  waiting for transfers between devices  33.1 us (27%)
  local copies, waits for them, and re-layouts  15 us (12%)
  between operations  13.4 us (11%)
  matrix products  8.17 us (7%)
    all_gather x1, blocking collectives, per_device(): lax.all_gather(adapter_up_factor, ('train', 'tp'), axis=2, tiled=True)  53.2 us
    all_gather x1, waiting for transfers between devices, build_shards(): return jnp.concatenate(lax.all_gather(slab_in, which_axis), axis=3)  32.4 us
    dot_general x1, matrix products, per_device(): jnp.einsum('eitd,eidh->eith', b_rows, build_shards(adapter_down_factor, (...  8.17 us
    reshape x1, local copies, waits for them, and re-layouts, build_shards(): return jnp.concatenate(lax.all_gather(slab_in, which_axis), axis=3)  7.38 us
    all_gather x1, local copies, waits for them, and re-layouts, build_shards(): return jnp.concatenate(lax.all_gather(slab_in, which_axis), axis=3)  6.59 us
  transfers between devices with their start and end apart: 1, of which 1 were waited for; matrix products, arithmetic and copies ran while one was open for 1% of the time, Pallas kernels for 0%

profile of v1, /device:TPU:0, one launch (start us, length us, event | category | flops | bytes accessed | tf_op | source)
XLA Modules:
  0.0 122.8 jit_solution(570417160657447954)
XLA Ops:
  6.5 0.0 all-gather.3.cloned.1.call-start
  6.5 0.7 all-gather.3.cloned.1.call-update
  7.3 0.9 copy.6
  8.2 53.2 %all_gather.9 = bf16[2,2,1024,64]{3,1,0,2:T(2,128)(2,1)S(1)} all-gather(bf16[2,2,64,64]{3,1,0,2:T(2,128)(2,1)S(1)} %copy.6), channel_id=1, replica_groups=mesh['train'=2,'tp'=8,'dp'=2] {'train','tp'}, dimensions={2}, use_global_device_ids=true | all-gather | bytes 557056 | tf_op jit(solution)/shard_map/all_gather | solution.py:15
  61.4 0.1 constant_dynamic-slice_fusion
  61.5 32.4 %all-gather.3.cloned.1.call-done = bf16[32,2,64,512]{3,2,1,0:T(8,128)(2,1)} async-done(((bf16[2,2,64,512]{3,2,1,0:T(8,128)(2,1)}), bf16[32,2,64,512]{3,2,1,0:T(8,128)(2,1)}) %all-gather.3.cloned.1.call-update) | async-done | bytes 4194320 | tf_op jit(solution)/shard_map/all_gather | solution.py:10
  93.8 6.6 %copy.13 = bf16[16,2,2,64,512]{4,0,3,2,1:T(8,128)(2,1)} copy(bf16[16,2,2,64,512]{4,3,2,1,0:T(8,128)(2,1)} %bitcast.8) | data formatting | bytes 8388608 | tf_op jit(solution)/shard_map/all_gather | solution.py:10
  100.4 7.4 %reshape.7 = bf16[2,2,64,8192]{3,2,1,0:T(8,128)(2,1)} reshape(bf16[2,2,64,16,512]{4,3,2,1,0:T(8,128)(2,1)} %bitcast.7) | data formatting | bytes 8388608 | tf_op jit(solution)/shard_map/reshape | solution.py:10
  107.8 8.2 %add_convert_fusion = bf16[2,2,128,8192]{3,2,1,0:T(8,128)(2,1)} fusion(bf16[2,2,128,8192]{3,2,1,0:T(8,128)(2,1)} %param.5, bf16[2,2,64,8192]{3,2,1,0:T(8,128)(2,1)} %reshape.7, bf16[2,2,128,64]{3,1,0,2:T(2,128)(2,1)S(1)} %constant_dynamic-slice_fusion), kind=kOutput, calls=%fused_computation | convolution fusion | flops 553648128 | bytes 21037056 | tf_op jit(solution)/shard_map/eitd,eidh->eith/dot_general | solution.py:19
Async XLA Ops:
  6.5 87.3 %all-gather.3.cloned.1.call-start = ((), (), s32[]{:S(2)}) async-start(), calls=%async_computation | async-start | bytes 4456448 | tf_op jit(solution)/shard_map/all_gather | solution.py:10
Sparse Core Ops, SparseCore 0:
  10.1 83.6 all-gather.2
